TPU v7x, 512 devices: a 4x2x32 block of a 4x8x32 slice. The times are simulated.
512 devices in a mesh: groups: 2 (over y), blk: 64 (over z, core), head: 4 (over x).
Axes of the slice: x: 4, y: 2, z: 32, core: 2. Of those that a mesh axis runs over, the one named last changes fastest.
The devices are a block of a 4x8x32 slice.
Arguments:
- queries: bfloat16 [4, 64, 8192], P('groups', 'blk', 'head'), parts along dimension 0, may hold values from -4.5 to 4.5
- stored_cache_keys: bfloat16 [4, 32768, 1024], P('groups', 'blk', 'head'), parts along dimension 0, may hold values from -4.5 to 4.5
- stored_cache_values: bfloat16 [4, 32768, 1024], P('groups', 'blk', 'head'), parts along dimension 0, may hold values from -6 to 6
- out_weight: bfloat16 [8192, 8192], P('head', 'blk'), may hold values from -3 to 3
- lengths: int32 [4], P('groups'), parts along dimension 0, may hold values from 16384 to 32768
Outputs:
- projected: bfloat16 [4, 64, 8192], P('groups', 'head', 'blk'), parts along dimension 0
There are 2 independent parts, one for each index of `groups`. A program takes and returns all parts, laid end to end along the dimension named above; an argument that names none is the same for every part. Nothing has to cross between parts.
All inputs are finite; a program needn't handle non-finite values.
Results may differ from a plain program's by a relative error of at most 0.0056.
Values may be sent and summed in bfloat16 or wider, within the bound.
No kernel may reach another device: no remote copies, remote signals or barrier semaphores. Data moves between devices by JAX's collectives and lax.ppermute only.
A program may use at most 64 MiB of HBM per device.

v0:
```python
import functools
import math

import jax
import jax.numpy as jnp
from jax import lax
from jax.experimental import pallas as pl
from jax.experimental.pallas import tpu as pltpu
from jax.sharding import Mesh
from jax.sharding import PartitionSpec as P


HEAD_DIMENSION = 128
CORES = 2
BLK = ("far", "near", "core")
NEAR = 2

masked_fill_value = -1e30
bf16 = jnp.bfloat16
f32 = jnp.float32


def in_vmem(kernel, shape, dtype, **more):
    def call(*arrays):
        scalar = [a.dtype == jnp.int32 for a in arrays]
        return pl.pallas_call(
            kernel,
            in_specs=[pl.BlockSpec(memory_space=pltpu.SMEM if s else pltpu.VMEM) for s in scalar],
            out_specs=pl.BlockSpec(memory_space=pltpu.VMEM),
            out_shape=pltpu.VMEM(shape, dtype),
            **more,
        )(*(a if s else pltpu.with_memory_space_constraint(a, pltpu.VMEM) for a, s in zip(arrays, scalar)))

    return call


def spread_kernel(queries, out):
    requests, dim = queries.shape[0], out.shape[2]
    group = out.shape[1] // requests
    wide = queries[...].astype(f32)
    for core in range(CORES):
        rows = [
            wide[r : r + 1, (core * group + h) * dim : (core * group + h + 1) * dim]
            for r in range(requests)
            for h in range(group)
        ]
        piece = jnp.concatenate(rows, axis=0).astype(bf16)
        for p in range(core, out.shape[0], CORES):
            out[p] = piece


def attention_kernel(place, lengths, queries, own_keys, own_values, other, out):
    new_count, requests, group, dim = queries.shape
    homes, per_home = out.shape[0], new_count // out.shape[0]
    span = own_keys.shape[1]
    rows = new_count * group
    far = homes // NEAR
    kept = per_home * requests
    scale = 1.0 / math.sqrt(dim)
    head = pl.ds(pl.multiple_of(place[0] * dim, dim), dim)
    lane = lax.broadcasted_iota(jnp.int32, (homes, group, dim), 2)
    stats = jnp.zeros((homes, group, dim), f32)
    home = lax.broadcasted_iota(jnp.int32, (rows, span), 0) // (group * per_home)
    token = (home % far * NEAR + home // far) * per_home
    token += lax.broadcasted_iota(jnp.int32, (rows, span), 0) // group % per_home
    column = lax.broadcasted_iota(jnp.int32, (rows, span), 1)
    for r in range(requests):
        q = queries[:, r].astype(f32).reshape(rows, dim).astype(bf16)
        last = lengths[r] - new_count
        keys = (own_keys[r, :, head], other[pl.ds(r * span, span), :])
        values = (own_values[r, :, head], other[pl.ds((requests + r) * span, span), :])
        scores = []
        for part in range(2):
            s = lax.dot_general(q, keys[part], (((1,), (1,)), ((), ())), preferred_element_type=f32)
            visible = column - token <= last - place[1 + part]
            scores.append(jnp.where(visible, s * scale, masked_fill_value))
        shift = jnp.max(jnp.maximum(*scores), axis=1, keepdims=True).astype(bf16).astype(f32)
        lowest = jnp.maximum(shift, 0.1 * masked_fill_value)
        weights = [jnp.exp(s - lowest) for s in scores]
        total = jnp.sum(weights[0] + weights[1], axis=1, keepdims=True)
        summed = sum(
            jnp.dot(w.astype(bf16), v, preferred_element_type=f32) for w, v in zip(weights, values)
        )
        high = total.astype(bf16).astype(f32)
        low = total - high
        summed = summed.reshape(homes, per_home, group, dim)
        for t in range(per_home):
            k = t * requests + r
            out[:, k] = summed[:, t].astype(bf16)
            for j, v in enumerate((shift, high, low)):
                v = v.reshape(homes, per_home, group, 1)[:, t]
                stats = jnp.where(lane == j * kept + k, v, stats)
    out[:, kept] = stats.astype(bf16)


def merged(parts):
    kept, dim = parts.shape[-3] - 1, parts.shape[-1]
    stats = parts[..., kept, :, :].astype(f32)
    shift = jnp.max(stats, axis=0)
    factor = jnp.exp(stats - shift[None])
    flat = stats.reshape(-1, dim)
    total = pltpu.roll(flat, dim - kept, 1) + pltpu.roll(flat, dim - 2 * kept, 1)
    total = jnp.sum(factor * total.reshape(stats.shape), axis=0)
    rows = [
        jnp.sum(parts[..., k, :, :].astype(f32) * factor[..., k : k + 1], axis=0) for k in range(kept)
    ]
    return rows, shift, total


def merge_near_kernel(parts, out):
    kept, dim = parts.shape[-3] - 1, parts.shape[-1]
    rows, shift, total = merged(parts)
    for k in range(kept):
        out[:, k] = rows[k].astype(bf16)
    high = total.astype(bf16).astype(f32)
    low = (total - high).reshape(-1, dim)
    high = pltpu.roll(high.reshape(-1, dim), kept, 1).reshape(shift.shape)
    low = pltpu.roll(low, 2 * kept, 1).reshape(shift.shape)
    lane = lax.broadcasted_iota(jnp.int32, shift.shape, len(shift.shape) - 1)
    out[:, kept] = jnp.where(lane < kept, shift, jnp.where(lane < 2 * kept, high, low)).astype(bf16)


def merge_far_kernel(parts, out):
    rows, _, total = merged(parts)
    for k, row in enumerate(rows):
        row = (row / total[:, k : k + 1]).astype(bf16)
        out[:, k] = jnp.broadcast_to(row[None], (out.shape[0], *row.shape))


def project_kernel(block, place, attention, weight, other, out, wide):
    pieces, per_piece, _ = out.shape
    inputs, dim = weight.shape[0] // CORES, attention.shape[1]
    group = inputs // dim
    rows = attention.shape[0] // group
    homes = wide.shape[0] // block
    for h in range(homes):
        source = h % NEAR * (homes // NEAR) + h // NEAR
        wide[h * block : (h + 1) * block] = attention[source * block : (source + 1) * block].astype(f32)
    left = jnp.concatenate(
        [wide[pl.ds(h, rows, stride=group), :].astype(bf16) for h in range(group)], axis=1
    )
    mine = weight[pl.ds(pl.multiple_of(place[0] * inputs, inputs), inputs), :]
    theirs = other[other.shape[0] - inputs :, :]
    for right, core in ((mine, place[0]), (theirs, 1 - place[0])):
        terms = jnp.dot(left, right, preferred_element_type=f32)
        for x in range(pieces // CORES):
            out[x * CORES + core] = terms[x * per_piece : (x + 1) * per_piece]


def exchanged(pieces, axes):
    flat = pieces.reshape(pieces.shape[0], -1, pieces.shape[-1])
    return lax.all_to_all(flat, axes, 0, 0, tiled=True).reshape(pieces.shape)


def shared(value, axis):
    return exchanged(jnp.broadcast_to(value[None], (lax.axis_size(axis), *value.shape)), axis)


def body(queries, stored_cache_keys, stored_cache_values, out_weight, lengths):
    requests, span, _ = stored_cache_keys.shape
    far_count, x_count = lax.axis_size("far"), lax.axis_size("head")
    z_count = far_count * NEAR
    new_count = queries.shape[1] * z_count * CORES
    dim = HEAD_DIMENSION
    group = queries.shape[2] // (CORES * dim)
    inputs = out_weight.shape[0] // CORES
    columns = out_weight.shape[1]
    z, core = lax.axis_index(("far", "near")), lax.axis_index("core")
    per_home = new_count // z_count
    kept = per_home * requests

    def head_of(cache, which):
        return lax.dynamic_slice_in_dim(cache, which * dim, dim, 2).reshape(requests * span, dim)

    leaving = jnp.concatenate(
        [
            head_of(stored_cache_keys, 1 - core),
            head_of(stored_cache_values, 1 - core),
            lax.dynamic_slice_in_dim(out_weight, (1 - core) * inputs, inputs, 0),
        ],
        axis=0,
    )
    arrived = lax.ppermute(leaving, "core", [(0, 1), (1, 0)])

    place = jnp.stack([core, (z * CORES + core) * span, (z * CORES + 1 - core) * span]).astype(jnp.int32)
    pieces = in_vmem(spread_kernel, (far_count * CORES, requests * group, dim), bf16)(queries.reshape(requests, -1))
    some_queries = lax.all_to_all(pieces, ("far", "core"), 0, 0, tiled=True)
    some_queries, arrived, place = lax.optimization_barrier((some_queries, arrived, place))
    all_queries = shared(some_queries, "near").reshape(new_count, requests, group, dim)


    partial = in_vmem(attention_kernel, (z_count, kept + 1, group, dim), bf16)(
        place, lengths, all_queries, stored_cache_keys, stored_cache_values, arrived
    )

    sent = partial.reshape(NEAR, far_count, *partial.shape[1:])
    partial = in_vmem(merge_near_kernel, sent.shape[1:], bf16)(exchanged(sent, "near"))
    own = in_vmem(merge_far_kernel, (far_count, kept, group, dim), bf16)(
        exchanged(partial, "far")
    )
    attention = shared(exchanged(own, "far"), "near")

    rows = z_count * kept
    terms = in_vmem(
        functools.partial(project_kernel, kept * group),
        (x_count * CORES, rows // x_count, columns),
        f32,
        scratch_shapes=[pltpu.VMEM((rows * group, dim), f32)],
    )(place, attention.reshape(rows * group, dim), out_weight, arrived)
    terms = lax.all_to_all(terms, ("head", "core"), 0, 0, tiled=True).sum(axis=0)
    terms = terms.reshape(-1, requests, columns).transpose(1, 0, 2)
    return terms.astype(bf16)


def solution(mesh):
    shape = mesh.devices.shape
    torus = Mesh(
        mesh.devices.reshape(shape[0], -1, NEAR, CORES, shape[2]),
        ("groups", "far", "near", "core", "head"),
    )
    return jax.shard_map(
        body,
        mesh=torus,
        in_specs=(
            P("groups", BLK, "head"),
            P("groups", BLK, "head"),
            P("groups", BLK, "head"),
            P("head", BLK),
            P("groups"),
        ),
        out_specs=P("groups", "head", BLK),
        check_vma=False,
    )
```

profile of v0, /device:TPU:33, one launch (start us, length us, event | category | flops | bytes accessed | tf_op | source)
XLA Modules:
  0.0 183.0 jit_solution(1883874661690700761)
XLA Ops:
  0.0 0.0 copy-start.1
  0.0 0.0 copy-start.3
  0.0 0.8 copy-done.3
  0.8 0.7 shard_map.55
  1.4 46.1 %all-to-all-start = ((bf16[32,16,128]{2,1,0:T(8,128)(2,1)}), bf16[32,16,128]{2,1,0:T(8,128)(2,1)S(1)}, u32[]{:S(2)}, u32[]{:S(2)}) async-start(bf16[32,16,128]{2,1,0:T(8,128)(2,1)} %shard_map.55), calls=%async_computation | async-start | bytes 262144 | tf_op jit(solution)/shard_map/all_to_all | solution.py:187
  47.5 1.0 constant_dynamic-slice_fusion
  48.5 0.0 copy-done.1
  48.5 1.0 constant_dynamic-slice_fusion.1
  49.5 0.1 pad_maximum_fusion
  49.6 0.0 copy-start.2
  49.6 2.8 %collective-permute-start = (bf16[3072,128]{1,0:T(8,128)(2,1)S(1)}, bf16[3072,128]{1,0:T(8,128)(2,1)S(1)}, u32[]{:S(2)}, u32[]{:S(2)}) collective-permute-start(bf16[3072,128]{1,0:T(8,128)(2,1)S(1)} %pad_maximum_fusion), channel_id=1, source_target_pairs={{0,4},{4,0},{1,5},{5,1},{2,6},{6,2},{3,7},{7,3},{8,12},{12,8},{9,1... | collective-permute-start | bytes 2359304 | tf_op jit(solution)/shard_map/ppermute | solution.py:183
  52.4 0.6 pad_add_fusion.place
  53.0 1.3 collective-permute-done.other
  54.3 23.1 %all-to-all-done = bf16[32,16,128]{2,1,0:T(8,128)(2,1)S(1)} async-done(((bf16[32,16,128]{2,1,0:T(8,128)(2,1)}), bf16[32,16,128]{2,1,0:T(8,128)(2,1)S(1)}, u32[]{:S(2)}, u32[]{:S(2)}) %all-to-all-start) | async-done | bytes 131104 | tf_op jit(solution)/shard_map/all_to_all | solution.py:187
  77.4 6.4 %all_to_all.35 = bf16[2,512,128]{2,1,0:T(8,128)(2,1)S(1)} all-to-all(bf16[2,512,128]{2,1,0:T(8,128)(2,1)S(1)} %broadcast_in_dim.16), channel_id=1, replica_groups=mesh['groups'=2,'far'=16,'near'=2,'core'=2,'head'=4] {'near'}, dimensions={0} | all-to-all | bytes 524288 | tf_op jit(solution)/shard_map/all_to_all | solution.py:152
  83.8 0.0 copy-done.2
  83.8 3.1 %shard_map.56 = bf16[32,5,8,128]{3,2,1,0:T(8,128)(2,1)S(1)} custom-call(s32[3]{0:T(128)} %pad_add_fusion.place, s32[2]{0:T(128)} %lengths.1, bf16[64,2,8,128]{3,2,1,0:T(8,128)(2,1)S(1)} %bitcast.21, bf16[2,512,256]{2,1,0:T(8,128)(2,1)S(1)} %copy-done.1, bf16[2,512,256]{2,1,0:T(8,128)(2,1)S(1)} %copy-done.2, bf16[3072,128]{1,0:T(8,128)(2,1)S(1)} %collective-permute-done.other), custom_call_target="tpu_custom_call" | custom-call | tf_op jit(solution)/shard_map/pallas_call | solution.py:26
  86.9 6.8 %all_to_all.36 = bf16[2,640,128]{2,1,0:T(8,128)(2,1)S(1)} all-to-all(bf16[2,640,128]{2,1,0:T(8,128)(2,1)S(1)} %bitcast.18), channel_id=1, replica_groups=mesh['groups'=2,'far'=16,'near'=2,'core'=2,'head'=4] {'near'}, dimensions={0} | all-to-all | bytes 655360 | tf_op jit(solution)/shard_map/all_to_all | solution.py:152
  93.7 0.3 shard_map.57
  94.0 26.4 %all_to_all.37 = bf16[16,40,128]{2,1,0:T(8,128)(2,1)S(1)} all-to-all(bf16[16,40,128]{2,1,0:T(8,128)(2,1)S(1)} %bitcast.23), channel_id=1, replica_groups=mesh['groups'=2,'far'=16,'near'=2,'core'=2,'head'=4] {'far'}, dimensions={0} | all-to-all | bytes 327680 | tf_op jit(solution)/shard_map/all_to_all | solution.py:152
  120.4 0.0 copy-start
  120.4 0.2 shard_map.58
  120.6 40.0 %all_to_all.38 = bf16[16,32,128]{2,1,0:T(8,128)(2,1)S(1)} all-to-all(bf16[16,32,128]{2,1,0:T(8,128)(2,1)S(1)} %bitcast.24), channel_id=1, replica_groups=mesh['groups'=2,'far'=16,'near'=2,'core'=2,'head'=4] {'far'}, dimensions={0} | all-to-all | bytes 262144 | tf_op jit(solution)/shard_map/all_to_all | solution.py:152
  160.6 6.4 %all_to_all.39 = bf16[2,512,128]{2,1,0:T(8,128)(2,1)S(1)} all-to-all(bf16[2,512,128]{2,1,0:T(8,128)(2,1)S(1)} %broadcast_in_dim.18), channel_id=1, replica_groups=mesh['groups'=2,'far'=16,'near'=2,'core'=2,'head'=4] {'near'}, dimensions={0} | all-to-all | bytes 524288 | tf_op jit(solution)/shard_map/all_to_all | solution.py:152
  167.0 0.0 copy-done
  167.0 1.0 shard_map.59
  168.0 14.4 %all_to_all.40 = f32[8,32,128]{2,1,0:T(8,128)S(1)} all-to-all(f32[8,32,128]{2,1,0:T(8,128)S(1)} %shard_map.59), channel_id=1, replica_groups=mesh['groups'=2,'far'=16,'near'=2,'core'=2,'head'=4] {'head','core'}, dimensions={0} | all-to-all | bytes 262144 | tf_op jit(solution)/shard_map/all_to_all | solution.py:210
  182.4 0.6 copy.6
  (3 shorter events, 0.1 us)
Async XLA Ops:
  0.0 48.5 %copy-start.1 = (bf16[2,512,256]{2,1,0:T(8,128)(2,1)S(1)}, bf16[2,512,256]{2,1,0:T(8,128)(2,1)}, u32[]{:S(2)}) copy-start(bf16[2,512,256]{2,1,0:T(8,128)(2,1)} %own_keys.1) | copy-start | bytes 1572868
  0.0 0.8 copy-start.3
  1.4 75.9 %all-to-all-start = ((bf16[32,16,128]{2,1,0:T(8,128)(2,1)}), bf16[32,16,128]{2,1,0:T(8,128)(2,1)S(1)}, u32[]{:S(2)}, u32[]{:S(2)}) async-start(bf16[32,16,128]{2,1,0:T(8,128)(2,1)} %shard_map.55), calls=%async_computation | async-start | bytes 262144 | tf_op jit(solution)/shard_map/all_to_all | solution.py:187
  49.6 34.2 %copy-start.2 = (bf16[2,512,256]{2,1,0:T(8,128)(2,1)S(1)}, bf16[2,512,256]{2,1,0:T(8,128)(2,1)}, u32[]{:S(2)}) copy-start(bf16[2,512,256]{2,1,0:T(8,128)(2,1)} %own_values.1) | copy-start | bytes 1572868
  49.6 4.7 %collective-permute-start = (bf16[3072,128]{1,0:T(8,128)(2,1)S(1)}, bf16[3072,128]{1,0:T(8,128)(2,1)S(1)}, u32[]{:S(2)}, u32[]{:S(2)}) collective-permute-start(bf16[3072,128]{1,0:T(8,128)(2,1)S(1)} %pad_maximum_fusion), channel_id=1, source_target_pairs={{0,4},{4,0},{1,5},{5,1},{2,6},{6,2},{3,7},{7,3},{8,12},{12,8},{9,1... | collective-permute-start | bytes 2359304 | tf_op jit(solution)/shard_map/ppermute | solution.py:183
  120.4 46.6 %copy-start = (bf16[2048,128]{1,0:T(8,128)(2,1)S(1)}, bf16[2048,128]{1,0:T(8,128)(2,1)}, u32[]{:S(2)}) copy-start(bf16[2048,128]{1,0:T(8,128)(2,1)} %weight.1) | copy-start | bytes 1572868
where the time goes:
time: 184 us; the launch traced here: 183 us
  blocking collectives  100 us (54%)
  starting transfers between devices  48.8 us (27%)
  waiting for transfers between devices  24.4 us (13%)
  Pallas kernels  5.22 us (3%)
  local copies, waits for them, and re-layouts  3.4 us (2%)
    all_to_all x5, blocking collectives, exchanged(): return lax.all_to_all(flat, axes, 0, 0, tiled=True).reshape(pieces.shape)  86 us
    all_to_all x1, starting transfers between devices, body(): some_queries = lax.all_to_all(pieces, ('far', 'core'), 0, 0, tiled=True)  46.1 us
    all_to_all x1, waiting for transfers between devices, body(): some_queries = lax.all_to_all(pieces, ('far', 'core'), 0, 0, tiled=True)  23.1 us
    all_to_all x1, blocking collectives, body(): lax.all_to_all(terms, ('head', 'core'), 0, 0, tiled=True).sum(axis=0)  14.4 us
    pallas_call x5, Pallas kernels, call(): pl.pallas_call(kernel, in_specs=[pl.BlockSpec(memory_space=pltpu.SMEM if...  5.22 us
  transfers between devices with their start and end apart: 2, of which 2 were waited for; matrix products, arithmetic and copies ran while one was open for 1% of the time, Pallas kernels for 0%

commit v1 on v0

v1 whole, which is shorter than its diff:
```python
import functools
import math

import jax
import jax.numpy as jnp
from jax import lax
from jax.experimental import pallas as pl
from jax.experimental.pallas import tpu as pltpu
from jax.sharding import Mesh
from jax.sharding import PartitionSpec as P


HEAD_DIMENSION = 128
CORES = 2
REQUESTS = 2
HALVES = 2
NEAR = HALVES * REQUESTS
NEAR_AXES = ("half", "req")
BLK = ("far", "half", "req", "core")

masked_fill_value = -1e30
bf16 = jnp.bfloat16
f32 = jnp.float32


def in_vmem(kernel, shape, dtype, **more):
    def call(*arrays):
        scalar = [a.dtype == jnp.int32 for a in arrays]
        return pl.pallas_call(
            kernel,
            in_specs=[pl.BlockSpec(memory_space=pltpu.SMEM if s else pltpu.VMEM) for s in scalar],
            out_specs=pl.BlockSpec(memory_space=pltpu.VMEM),
            out_shape=pltpu.VMEM(shape, dtype),
            **more,
        )(*(a if s else pltpu.with_memory_space_constraint(a, pltpu.VMEM) for a, s in zip(arrays, scalar)))

    return call


def spread_kernel(queries, out):
    requests, dim = queries.shape[0], out.shape[2]
    group = out.shape[1] // requests
    wide = queries[...].astype(f32)
    for core in range(CORES):
        rows = [
            wide[r : r + 1, (core * group + h) * dim : (core * group + h + 1) * dim]
            for r in range(requests)
            for h in range(group)
        ]
        piece = jnp.concatenate(rows, axis=0).astype(bf16)
        for p in range(core, out.shape[0], CORES):
            out[p] = piece


def attention_kernel(place, lengths, queries, own_keys, own_values, second, third, fourth, out):
    new_count, group, dim = queries.shape
    halves, far, kept = out.shape[0], out.shape[1], out.shape[2] - 1
    span = own_keys.shape[1]
    rows = new_count * group
    inner = NEAR // halves
    scale = 1.0 / math.sqrt(dim)
    core, request = place[0], place[1]
    head = pl.ds(pl.multiple_of(core * dim, dim), dim)
    row = lax.broadcasted_iota(jnp.int32, (rows, span), 0) // group
    token = row // CORES % far * (NEAR * CORES) + row // (far * CORES) * CORES + row % CORES
    ahead = lax.broadcasted_iota(jnp.int32, (rows, span), 1) - token
    q = queries[...].astype(f32).reshape(rows, dim).astype(bf16)
    last = lengths[request] - new_count
    keys = [own_keys[request, :, head]] + [other[:span, :] for other in (second, third, fourth)]
    values = [own_values[request, :, head]]
    values += [other[span : 2 * span, :] for other in (second, third, fourth)]
    scores = []
    for part, k in enumerate(keys):
        s = lax.dot_general(q, k, (((1,), (1,)), ((), ())), preferred_element_type=f32)
        scores.append(jnp.where(ahead <= last - place[2 + part], s * scale, masked_fill_value))
    shift = jnp.max(functools.reduce(jnp.maximum, scores), axis=1, keepdims=True)
    shift = shift.astype(bf16).astype(f32)
    lowest = jnp.maximum(shift, 0.1 * masked_fill_value)
    weights = [jnp.exp(s - lowest) for s in scores]
    total = jnp.sum(sum(weights), axis=1, keepdims=True)
    summed = sum(
        jnp.dot(w.astype(bf16), v, preferred_element_type=f32) for w, v in zip(weights, values)
    )
    high = total.astype(bf16).astype(f32)
    low = total - high
    lane = lax.broadcasted_iota(jnp.int32, (halves, far, group, dim), 3)
    stats = jnp.zeros((halves, far, group, dim), f32)
    summed = summed.reshape(halves, inner, far, CORES, group, dim)
    for k in range(kept):
        n, c = k // CORES, k % CORES
        out[:, :, k] = summed[:, n, :, c].astype(bf16)
        for j, v in enumerate((shift, high, low)):
            v = v.reshape(halves, inner, far, CORES, group, 1)[:, n, :, c]
            stats = jnp.where(lane == j * kept + k, v, stats)
    out[:, :, kept] = stats.astype(bf16)


def merged(parts):
    kept, dim = parts.shape[-3] - 1, parts.shape[-1]
    stats = parts[..., kept, :, :].astype(f32)
    shift = jnp.max(stats, axis=0)
    factor = jnp.exp(stats - shift[None])
    flat = stats.reshape(-1, dim)
    total = pltpu.roll(flat, dim - kept, 1) + pltpu.roll(flat, dim - 2 * kept, 1)
    total = jnp.sum(factor * total.reshape(stats.shape), axis=0)
    rows = [
        jnp.sum(parts[..., k, :, :].astype(f32) * factor[..., k : k + 1], axis=0) for k in range(kept)
    ]
    return rows, shift, total


def merge_near_kernel(parts, out):
    kept, dim = parts.shape[-3] - 1, parts.shape[-1]
    rows, shift, total = merged(parts)
    for k in range(kept):
        out[:, k] = rows[k].astype(bf16)
    high = total.astype(bf16).astype(f32)
    low = (total - high).reshape(-1, dim)
    high = pltpu.roll(high.reshape(-1, dim), kept, 1).reshape(shift.shape)
    low = pltpu.roll(low, 2 * kept, 1).reshape(shift.shape)
    lane = lax.broadcasted_iota(jnp.int32, shift.shape, len(shift.shape) - 1)
    out[:, kept] = jnp.where(lane < kept, shift, jnp.where(lane < 2 * kept, high, low)).astype(bf16)


def merge_far_kernel(parts, out):
    rows, _, total = merged(parts)
    for k, row in enumerate(rows):
        row = (row / total[:, k : k + 1]).astype(bf16)
        out[:, k] = jnp.broadcast_to(row[None], (out.shape[0], *row.shape))


def project_kernel(place, attention, weight, other, out, wide):
    pieces, per_piece, _ = out.shape
    inputs, dim = weight.shape[0] // CORES, attention.shape[1]
    group = inputs // dim
    rows = attention.shape[0] // group
    kept = NEAR // HALVES * CORES
    far_count = rows // (NEAR * kept)
    for source in range(rows):
        half, req = source // (REQUESTS * far_count * kept), source // (far_count * kept) % REQUESTS
        far, k = source // kept % far_count, source % kept
        z = far * NEAR + half * (NEAR // HALVES) + k // CORES
        at = (z * CORES + k % CORES) * REQUESTS + req
        wide[at * group : (at + 1) * group] = attention[source * group : (source + 1) * group].astype(f32)
    left = jnp.concatenate(
        [wide[pl.ds(h, rows, stride=group), :].astype(bf16) for h in range(group)], axis=1
    )
    mine = weight[pl.ds(pl.multiple_of(place[0] * inputs, inputs), inputs), :]
    theirs = other[other.shape[0] - inputs :, :]
    for right, core in ((mine, place[0]), (theirs, 1 - place[0])):
        terms = jnp.dot(left, right, preferred_element_type=f32)
        for x in range(pieces // CORES):
            out[x * CORES + core] = terms[x * per_piece : (x + 1) * per_piece]


def exchanged(pieces, axes):
    flat = pieces.reshape(pieces.shape[0], -1, pieces.shape[-1])
    return lax.all_to_all(flat, axes, 0, 0, tiled=True).reshape(pieces.shape)


def shared(value, axis):
    return exchanged(jnp.broadcast_to(value[None], (lax.axis_size(axis), *value.shape)), axis)


def body(queries, stored_cache_keys, stored_cache_values, out_weight, lengths):
    requests, span, _ = stored_cache_keys.shape
    far_count, x_count = lax.axis_size("far"), lax.axis_size("head")
    z_count = far_count * NEAR
    new_count = queries.shape[1] * z_count * CORES
    dim = HEAD_DIMENSION
    group = queries.shape[2] // (CORES * dim)
    inputs = out_weight.shape[0] // CORES
    columns = out_weight.shape[1]
    z, core, req = lax.axis_index(("far", *NEAR_AXES)), lax.axis_index("core"), lax.axis_index("req")
    kept = NEAR // HALVES * CORES
    rows = new_count * requests

    def caches(request, head):
        sizes = (1, span, dim)
        both = (stored_cache_keys, stored_cache_values)
        return [lax.dynamic_slice(a, (request, 0, head * dim), sizes).reshape(span, dim) for a in both]

    def swapped(arrays, flip_req, flip_core):
        pairs = [
            (r * CORES + c, (r ^ flip_req) * CORES + (c ^ flip_core))
            for r in range(REQUESTS)
            for c in range(CORES)
        ]
        return lax.ppermute(jnp.concatenate(arrays, axis=0), ("req", "core"), pairs)

    theirs = lax.dynamic_slice_in_dim(out_weight, (1 - core) * inputs, inputs, 0)
    second = swapped([*caches(req, 1 - core), theirs], 0, 1)
    third = swapped(caches(1 - req, core), 1, 0)
    fourth = swapped(caches(1 - req, 1 - core), 1, 1)

    other_z = z + 1 - 2 * req
    first = [z * CORES + core, z * CORES + 1 - core, other_z * CORES + core, other_z * CORES + 1 - core]
    place = jnp.stack([core, req, *(b * span for b in first)]).astype(jnp.int32)
    pieces = in_vmem(spread_kernel, (far_count * CORES, requests * group, dim), bf16)(queries.reshape(requests, -1))
    some_queries = lax.all_to_all(pieces, ("far", "core"), 0, 0, tiled=True)
    some_queries, second, third, fourth, place = lax.optimization_barrier(
        (some_queries, second, third, fourth, place)
    )
    pieces = some_queries.reshape(-1, requests, group, dim).transpose(1, 0, 2, 3)
    pieces = jnp.broadcast_to(pieces[None], (HALVES, *pieces.shape)).reshape(NEAR, *pieces.shape[1:])
    all_queries = exchanged(pieces, NEAR_AXES).reshape(new_count, group, dim)

    partial = in_vmem(attention_kernel, (HALVES, far_count, kept + 1, group, dim), bf16)(
        place, lengths, all_queries, stored_cache_keys, stored_cache_values, second, third, fourth
    )
    partial = in_vmem(merge_near_kernel, partial.shape[1:], bf16)(exchanged(partial, "half"))
    own = in_vmem(merge_far_kernel, (far_count, kept, group, dim), bf16)(
        exchanged(partial, "far")
    )
    attention = shared(exchanged(own, "far"), NEAR_AXES)

    terms = in_vmem(
        project_kernel,
        (x_count * CORES, rows // x_count, columns),
        f32,
        scratch_shapes=[pltpu.VMEM((rows * group, dim), f32)],
    )(place, attention.reshape(rows * group, dim), out_weight, second)
    terms = lax.all_to_all(terms, ("head", "core"), 0, 0, tiled=True).sum(axis=0)
    terms = terms.reshape(-1, requests, columns).transpose(1, 0, 2)
    return terms.astype(bf16)


def solution(mesh):
    shape = mesh.devices.shape
    torus = Mesh(
        mesh.devices.reshape(shape[0], -1, HALVES, REQUESTS, CORES, shape[2]),
        ("groups", *BLK, "head"),
    )
    return jax.shard_map(
        body,
        mesh=torus,
        in_specs=(
            P("groups", BLK, "head"),
            P("groups", BLK, "head"),
            P("groups", BLK, "head"),
            P("head", BLK),
            P("groups"),
        ),
        out_specs=P("groups", "head", BLK),
        check_vma=False,
    )
```

time: 184 us -> 185 us (level)
  waiting for transfers between devices: 24.4 us -> 19.8 us
  starting transfers between devices: 48.8 us -> 52.9 us
  blocking collectives: 100 us -> 102 us
    ppermute x1 -> x3, starting transfers between devices: 2.77 us -> 49.3 us  [swapped(): return lax.ppermute(jnp.concatenate(arrays, axis=0), ('req', 'core'), pairs)]
    all_to_all x1, starting transfers between devices: 46.1 us -> 3.66 us  [body(): some_queries = lax.all_to_all(pieces, ('far', 'core'), 0, 0, tiled=True)]
    all_to_all x1, waiting for transfers between devices: 23.1 us -> 6.23 us  [body(): some_queries = lax.all_to_all(pieces, ('far', 'core'), 0, 0, tiled=True)]
    ppermute x1 -> x3, waiting for transfers between devices: 1.29 us -> 13.6 us  [swapped(): return lax.ppermute(jnp.concatenate(arrays, axis=0), ('req', 'core'), pairs)]
    all_to_all x1, blocking collectives: 14.4 us -> 17.4 us  [body(): lax.all_to_all(terms, ('head', 'core'), 0, 0, tiled=True).sum(axis=0)]
  transfers between devices with their start and end apart: 2 -> 4, of which waited for: 2 -> 3; matrix products, arithmetic and copies ran while one was open for 1% -> 0% of each run, Pallas kernels for 0% -> 0%
where the time goes in v1:
time: 185 us
  blocking collectives  102 us (55%)
  starting transfers between devices  52.9 us (29%)
  waiting for transfers between devices  19.8 us (11%)
  Pallas kernels  5.84 us (3%)
  local copies, waits for them, and re-layouts  3.54 us (2%)
    all_to_all x5, blocking collectives, exchanged(): return lax.all_to_all(flat, axes, 0, 0, tiled=True).reshape(pieces.shape)  84.9 us
    ppermute x3, starting transfers between devices, swapped(): return lax.ppermute(jnp.concatenate(arrays, axis=0), ('req', 'core'), pairs)  49.3 us
    all_to_all x1, blocking collectives, body(): lax.all_to_all(terms, ('head', 'core'), 0, 0, tiled=True).sum(axis=0)  17.4 us
    ppermute x3, waiting for transfers between devices, swapped(): return lax.ppermute(jnp.concatenate(arrays, axis=0), ('req', 'core'), pairs)  13.6 us
    all_to_all x1, waiting for transfers between devices, body(): some_queries = lax.all_to_all(pieces, ('far', 'core'), 0, 0, tiled=True)  6.23 us
    pallas_call x5, Pallas kernels, call(): pl.pallas_call(kernel, in_specs=[pl.BlockSpec(memory_space=pltpu.SMEM if...  5.84 us
  transfers between devices with their start and end apart: 4, of which 3 were waited for; matrix products, arithmetic and copies ran while one was open for 0% of the time, Pallas kernels for 0%

profile of v1, /device:TPU:33, one launch (start us, length us, event | category | flops | bytes accessed | tf_op | source)
XLA Modules:
  0.0 184.7 jit_solution(18116204042819029874)
XLA Ops:
  0.0 0.0 copy-start
  0.0 1.0 constant_dynamic-slice_fusion
  1.0 0.1 copy-done
  1.1 1.1 dynamic-slice_bitcast_fusion
  2.2 0.0 copy-start.3
  2.3 43.4 %collective-permute-start = (bf16[2048,128]{1,0:T(8,128)(2,1)S(1)}, bf16[2048,128]{1,0:T(8,128)(2,1)S(1)}, u32[]{:S(2)}, u32[]{:S(2)}) collective-permute-start(bf16[2048,128]{1,0:T(8,128)(2,1)S(1)} %pad_maximum_fusion), channel_id=1, source_target_pairs={{0,4},{4,0},{8,12},{12,8},{1,5},{5,1},{9,13},{13,9},{2,6},{6,2},{1... | collective-permute-start | bytes 1572872 | tf_op jit(solution)/shard_map/ppermute | solution.py:189
  45.7 0.0 copy-done.3
  45.7 0.6 shard_map.55
  46.3 3.7 %all-to-all-start = ((bf16[16,16,128]{2,1,0:T(8,128)(2,1)}), bf16[16,16,128]{2,1,0:T(8,128)(2,1)S(1)}, u32[]{:S(2)}, u32[]{:S(2)}) async-start(bf16[16,16,128]{2,1,0:T(8,128)(2,1)} %shard_map.55), calls=%async_computation | async-start | bytes 131072 | tf_op jit(solution)/shard_map/all_to_all | solution.py:200
  50.0 3.4 %collective-permute-start.1 = (bf16[1024,128]{1,0:T(8,128)(2,1)S(1)}, bf16[1024,128]{1,0:T(8,128)(2,1)S(1)}, u32[]{:S(2)}, u32[]{:S(2)}) collective-permute-start(bf16[1024,128]{1,0:T(8,128)(2,1)S(1)} %pad_maximum_fusion.1), channel_id=1, source_target_pairs={{0,8},{4,12},{8,0},{12,4},{1,9},{5,13},{9,1},{13,5},{2,10},{6,14},... | collective-permute-start | bytes 786440 | tf_op jit(solution)/shard_map/ppermute | solution.py:189
  53.4 0.0 copy-start.1
  53.5 2.5 %collective-permute-start.2 = (bf16[1024,128]{1,0:T(8,128)(2,1)S(1)}, bf16[1024,128]{1,0:T(8,128)(2,1)S(1)}, u32[]{:S(2)}, u32[]{:S(2)}) collective-permute-start(bf16[1024,128]{1,0:T(8,128)(2,1)S(1)} %pad_maximum_fusion.2), channel_id=1, source_target_pairs={{0,12},{4,8},{8,4},{12,0},{1,13},{5,9},{9,5},{13,1},{2,14},{6,10},... | collective-permute-start | bytes 786440 | tf_op jit(solution)/shard_map/ppermute | solution.py:189
  56.0 0.6 stack.27.place
  56.6 6.1 %collective-permute-done.1.third = bf16[1024,128]{1,0:T(8,128)(2,1)S(1)} collective-permute-done((bf16[1024,128]{1,0:T(8,128)(2,1)S(1)}, bf16[1024,128]{1,0:T(8,128)(2,1)S(1)}, u32[]{:S(2)}, u32[]{:S(2)}) %collective-permute-start.1) | collective-permute-done | bytes 262176 | tf_op jit(solution)/shard_map/ppermute | solution.py:189
  62.8 7.5 %collective-permute-done.2.fourth = bf16[1024,128]{1,0:T(8,128)(2,1)S(1)} collective-permute-done((bf16[1024,128]{1,0:T(8,128)(2,1)S(1)}, bf16[1024,128]{1,0:T(8,128)(2,1)S(1)}, u32[]{:S(2)}, u32[]{:S(2)}) %collective-permute-start.2) | collective-permute-done | bytes 262176 | tf_op jit(solution)/shard_map/ppermute | solution.py:189
  70.2 6.2 %all-to-all-done = bf16[16,16,128]{2,1,0:T(8,128)(2,1)S(1)} async-done(((bf16[16,16,128]{2,1,0:T(8,128)(2,1)}), bf16[16,16,128]{2,1,0:T(8,128)(2,1)S(1)}, u32[]{:S(2)}, u32[]{:S(2)}) %all-to-all-start) | async-done | bytes 65568 | tf_op jit(solution)/shard_map/all_to_all | solution.py:200
  76.5 0.0 collective-permute-done.second.other
  76.5 8.3 %all_to_all.35 = bf16[4,128,128]{2,1,0:T(8,128)(2,1)S(1)} all-to-all(bf16[4,128,128]{2,1,0:T(8,128)(2,1)S(1)} %bitcast.42), channel_id=1, replica_groups=mesh['groups'=2,'far'=8,'half'=2,'req'=2,'core'=2,'head'=4] {'half','req'}, dimensions={0} | all-to-all | bytes 262144 | tf_op jit(solution)/shard_map/all_to_all | solution.py:158
  84.8 0.0 copy-done.1
  84.8 3.9 %shard_map.56 = bf16[2,8,5,8,128]{4,3,2,1,0:T(8,128)(2,1)S(1)} custom-call(s32[6]{0:T(128)} %stack.27.place, s32[2]{0:T(128)} %lengths.1, bf16[64,8,128]{2,1,0:T(8,128)(2,1)S(1)} %bitcast.37, bf16[2,512,256]{2,1,0:T(8,128)(2,1)S(1)} %copy-done, bf16[2,512,256]{2,1,0:T(8,128)(2,1)S(1)} %copy-done.1, bf16[2048,128]{1,0:T(8,128)(2,1)S(1)} %collective-permute-done.second.other, ...), custom_call_target="tpu_custom_call" | custom-call | tf_op jit(solution)/shard_map/pallas_call | solution.py:29
  88.7 7.1 %all_to_all.36 = bf16[2,320,128]{2,1,0:T(8,128)(2,1)S(1)} all-to-all(bf16[2,320,128]{2,1,0:T(8,128)(2,1)S(1)} %bitcast.35), channel_id=1, replica_groups=mesh['groups'=2,'far'=8,'half'=2,'req'=2,'core'=2,'head'=4] {'half'}, dimensions={0} | all-to-all | bytes 327680 | tf_op jit(solution)/shard_map/all_to_all | solution.py:158
  95.8 0.2 shard_map.57
  95.9 35.5 %all_to_all.37 = bf16[8,40,128]{2,1,0:T(8,128)(2,1)S(1)} all-to-all(bf16[8,40,128]{2,1,0:T(8,128)(2,1)S(1)} %bitcast.39), channel_id=1, replica_groups=mesh['groups'=2,'far'=8,'half'=2,'req'=2,'core'=2,'head'=4] {'far'}, dimensions={0} | all-to-all | bytes 163840 | tf_op jit(solution)/shard_map/all_to_all | solution.py:158
  131.4 0.2 shard_map.58
  131.6 0.0 copy-start.2
  131.6 25.7 %all_to_all.38 = bf16[8,32,128]{2,1,0:T(8,128)(2,1)S(1)} all-to-all(bf16[8,32,128]{2,1,0:T(8,128)(2,1)S(1)} %bitcast.40), channel_id=1, replica_groups=mesh['groups'=2,'far'=8,'half'=2,'req'=2,'core'=2,'head'=4] {'far'}, dimensions={0} | all-to-all | bytes 131072 | tf_op jit(solution)/shard_map/all_to_all | solution.py:158
  157.3 8.4 %all_to_all.39 = bf16[4,256,128]{2,1,0:T(8,128)(2,1)S(1)} all-to-all(bf16[4,256,128]{2,1,0:T(8,128)(2,1)S(1)} %broadcast_in_dim.15), channel_id=1, replica_groups=mesh['groups'=2,'far'=8,'half'=2,'req'=2,'core'=2,'head'=4] {'half','req'}, dimensions={0} | all-to-all | bytes 524288 | tf_op jit(solution)/shard_map/all_to_all | solution.py:158
  165.7 0.0 copy-done.2
  165.7 1.0 shard_map.59
  166.7 17.4 %all_to_all.40 = f32[8,32,128]{2,1,0:T(8,128)S(1)} all-to-all(f32[8,32,128]{2,1,0:T(8,128)S(1)} %shard_map.59), channel_id=1, replica_groups=mesh['groups'=2,'far'=8,'half'=2,'req'=2,'core'=2,'head'=4] {'head','core'}, dimensions={0} | all-to-all | bytes 262144 | tf_op jit(solution)/shard_map/all_to_all | solution.py:223
  184.1 0.6 copy.8
  (7 shorter events, 0.1 us)
Async XLA Ops:
  0.0 1.1 copy-start
  2.2 43.4 %copy-start.3 = (bf16[2,1,2048]{2,0,1:T(2,128)(2,1)S(1)}, bf16[2,1,2048]{2,0,1:T(2,128)(2,1)}, u32[]{:S(2)}) copy-start(bf16[2,1,2048]{2,0,1:T(2,128)(2,1)} %param.5) | copy-start | bytes 24580
  2.3 74.2 %collective-permute-start = (bf16[2048,128]{1,0:T(8,128)(2,1)S(1)}, bf16[2048,128]{1,0:T(8,128)(2,1)S(1)}, u32[]{:S(2)}, u32[]{:S(2)}) collective-permute-start(bf16[2048,128]{1,0:T(8,128)(2,1)S(1)} %pad_maximum_fusion), channel_id=1, source_target_pairs={{0,4},{4,0},{8,12},{12,8},{1,5},{5,1},{9,13},{13,9},{2,6},{6,2},{1... | collective-permute-start | bytes 1572872 | tf_op jit(solution)/shard_map/ppermute | solution.py:189
  46.3 30.2 %all-to-all-start = ((bf16[16,16,128]{2,1,0:T(8,128)(2,1)}), bf16[16,16,128]{2,1,0:T(8,128)(2,1)S(1)}, u32[]{:S(2)}, u32[]{:S(2)}) async-start(bf16[16,16,128]{2,1,0:T(8,128)(2,1)} %shard_map.55), calls=%async_computation | async-start | bytes 131072 | tf_op jit(solution)/shard_map/all_to_all | solution.py:200
  50.0 12.8 %collective-permute-start.1 = (bf16[1024,128]{1,0:T(8,128)(2,1)S(1)}, bf16[1024,128]{1,0:T(8,128)(2,1)S(1)}, u32[]{:S(2)}, u32[]{:S(2)}) collective-permute-start(bf16[1024,128]{1,0:T(8,128)(2,1)S(1)} %pad_maximum_fusion.1), channel_id=1, source_target_pairs={{0,8},{4,12},{8,0},{12,4},{1,9},{5,13},{9,1},{13,5},{2,10},{6,14},... | collective-permute-start | bytes 786440 | tf_op jit(solution)/shard_map/ppermute | solution.py:189
  53.4 31.3 %copy-start.1 = (bf16[2,512,256]{2,1,0:T(8,128)(2,1)S(1)}, bf16[2,512,256]{2,1,0:T(8,128)(2,1)}, u32[]{:S(2)}) copy-start(bf16[2,512,256]{2,1,0:T(8,128)(2,1)} %own_values.1) | copy-start | bytes 1572868
  53.5 16.8 %collective-permute-start.2 = (bf16[1024,128]{1,0:T(8,128)(2,1)S(1)}, bf16[1024,128]{1,0:T(8,128)(2,1)S(1)}, u32[]{:S(2)}, u32[]{:S(2)}) collective-permute-start(bf16[1024,128]{1,0:T(8,128)(2,1)S(1)} %pad_maximum_fusion.2), channel_id=1, source_target_pairs={{0,12},{4,8},{8,4},{12,0},{1,13},{5,9},{9,5},{13,1},{2,14},{6,10},... | collective-permute-start | bytes 786440 | tf_op jit(solution)/shard_map/ppermute | solution.py:189
  131.6 34.1 %copy-start.2 = (bf16[2048,128]{1,0:T(8,128)(2,1)S(1)}, bf16[2048,128]{1,0:T(8,128)(2,1)}, u32[]{:S(2)}) copy-start(bf16[2048,128]{1,0:T(8,128)(2,1)} %weight.1) | copy-start | bytes 1572868

commit v2 on v1

--- a/solution.py
+++ b/solution.py
@@ -52,7 +52,7 @@
             out[p] = piece
 
 
-def attention_kernel(place, lengths, queries, own_keys, own_values, second, third, fourth, out):
+def attention_kernel(place, lengths, queries, own_keys, own_values, lent, other, out):
     new_count, group, dim = queries.shape
     halves, far, kept = out.shape[0], out.shape[1], out.shape[2] - 1
     span = own_keys.shape[1]
@@ -66,9 +66,9 @@
     ahead = lax.broadcasted_iota(jnp.int32, (rows, span), 1) - token
     q = queries[...].astype(f32).reshape(rows, dim).astype(bf16)
     last = lengths[request] - new_count
-    keys = [own_keys[request, :, head]] + [other[:span, :] for other in (second, third, fourth)]
-    values = [own_values[request, :, head]]
-    values += [other[span : 2 * span, :] for other in (second, third, fourth)]
+    keys = [own_keys[request, :, head], other[:span, :], lent[:span, head], other[2 * span : 3 * span, :]]
+    values = [own_values[request, :, head], other[span : 2 * span, :]]
+    values += [lent[span:, head], other[3 * span : 4 * span, :]]
     scores = []
     for part, k in enumerate(keys):
         s = lax.dot_general(q, k, (((1,), (1,)), ((), ())), preferred_element_type=f32)
@@ -175,38 +175,31 @@
     kept = NEAR // HALVES * CORES
     rows = new_count * requests
 
-    def caches(request, head):
-        sizes = (1, span, dim)
-        both = (stored_cache_keys, stored_cache_values)
-        return [lax.dynamic_slice(a, (request, 0, head * dim), sizes).reshape(span, dim) for a in both]
-
-    def swapped(arrays, flip_req, flip_core):
-        pairs = [
-            (r * CORES + c, (r ^ flip_req) * CORES + (c ^ flip_core))
-            for r in range(REQUESTS)
-            for c in range(CORES)
-        ]
-        return lax.ppermute(jnp.concatenate(arrays, axis=0), ("req", "core"), pairs)
-
+    def of_request(cache, request):
+        return lax.dynamic_index_in_dim(cache, request, 0, keepdims=False)
+
+    def head_of(cache, head):
+        return lax.dynamic_slice_in_dim(cache, head * dim, dim, 1)
+
+    caches = (stored_cache_keys, stored_cache_values)
+    leaving = jnp.concatenate([of_request(a, 1 - req) for a in caches], axis=0)
+    lent = lax.ppermute(leaving, "req", [(0, 1), (1, 0)])
     theirs = lax.dynamic_slice_in_dim(out_weight, (1 - core) * inputs, inputs, 0)
-    second = swapped([*caches(req, 1 - core), theirs], 0, 1)
-    third = swapped(caches(1 - req, core), 1, 0)
-    fourth = swapped(caches(1 - req, 1 - core), 1, 1)
+    leaving = [head_of(a, 1 - core) for a in (*(of_request(a, req) for a in caches), lent)]
+    other = lax.ppermute(jnp.concatenate([*leaving, theirs], axis=0), "core", [(0, 1), (1, 0)])
 
     other_z = z + 1 - 2 * req
     first = [z * CORES + core, z * CORES + 1 - core, other_z * CORES + core, other_z * CORES + 1 - core]
     place = jnp.stack([core, req, *(b * span for b in first)]).astype(jnp.int32)
     pieces = in_vmem(spread_kernel, (far_count * CORES, requests * group, dim), bf16)(queries.reshape(requests, -1))
     some_queries = lax.all_to_all(pieces, ("far", "core"), 0, 0, tiled=True)
-    some_queries, second, third, fourth, place = lax.optimization_barrier(
-        (some_queries, second, third, fourth, place)
-    )
+    some_queries, lent, other, place = lax.optimization_barrier((some_queries, lent, other, place))
     pieces = some_queries.reshape(-1, requests, group, dim).transpose(1, 0, 2, 3)
     pieces = jnp.broadcast_to(pieces[None], (HALVES, *pieces.shape)).reshape(NEAR, *pieces.shape[1:])
     all_queries = exchanged(pieces, NEAR_AXES).reshape(new_count, group, dim)
 
     partial = in_vmem(attention_kernel, (HALVES, far_count, kept + 1, group, dim), bf16)(
-        place, lengths, all_queries, stored_cache_keys, stored_cache_values, second, third, fourth
+        place, lengths, all_queries, stored_cache_keys, stored_cache_values, lent, other
     )
     partial = in_vmem(merge_near_kernel, partial.shape[1:], bf16)(exchanged(partial, "half"))
     own = in_vmem(merge_far_kernel, (far_count, kept, group, dim), bf16)(
@@ -219,7 +212,7 @@
         (x_count * CORES, rows // x_count, columns),
         f32,
         scratch_shapes=[pltpu.VMEM((rows * group, dim), f32)],
-    )(place, attention.reshape(rows * group, dim), out_weight, second)
+    )(place, attention.reshape(rows * group, dim), out_weight, other)
     terms = lax.all_to_all(terms, ("head", "core"), 0, 0, tiled=True).sum(axis=0)
     terms = terms.reshape(-1, requests, columns).transpose(1, 0, 2)
     return terms.astype(bf16)

time: 185 us -> 191 us (1.032)
  waiting for transfers between devices: 19.8 us -> 32 us
  blocking collectives: 102 us -> 92.7 us
  starting transfers between devices: 52.9 us -> 56.3 us
    all_to_all x1, waiting for transfers between devices: 6.23 us -> 25.6 us  [body(): some_queries = lax.all_to_all(pieces, ('far', 'core'), 0, 0, tiled=True)]
    ppermute x3 -> x2, waiting for transfers between devices: 13.6 us -> 6.32 us  [the longest x1 6.32 us: body(): lent = lax.ppermute(leaving, 'req', [(0, 1), (1, 0)])]
    all_to_all x5, blocking collectives: 84.9 us -> 78 us  [exchanged(): return lax.all_to_all(flat, axes, 0, 0, tiled=True).reshape(pieces.shape)]
    all_to_all x1, starting transfers between devices: 3.66 us -> 8.26 us  [body(): some_queries = lax.all_to_all(pieces, ('far', 'core'), 0, 0, tiled=True)]
    all_to_all x1, blocking collectives: 17.4 us -> 14.7 us  [body(): lax.all_to_all(terms, ('head', 'core'), 0, 0, tiled=True).sum(axis=0)]
    ppermute x3 -> x2, starting transfers between devices: 49.3 us -> 48 us  [the longest x1 42.6 us: body(): lax.ppermute(jnp.concatenate([*leaving, theirs], axis=0), 'core', [(0, 1)...]
  transfers between devices with their start and end apart: 4 -> 3, of which waited for: 3 -> 2; matrix products, arithmetic and copies ran while one was open for 0% -> 0% of each run, Pallas kernels for 0% -> 0%
where the time goes in v2:
time: 191 us
  blocking collectives  92.7 us (49%)
  starting transfers between devices  56.3 us (29%)
  waiting for transfers between devices  32 us (17%)
  Pallas kernels  5.85 us (3%)
  local copies, waits for them, and re-layouts  2.55 us (1%)
    all_to_all x5, blocking collectives, exchanged(): return lax.all_to_all(flat, axes, 0, 0, tiled=True).reshape(pieces.shape)  78 us
    ppermute x1, starting transfers between devices, body(): lax.ppermute(jnp.concatenate([*leaving, theirs], axis=0), 'core', [(0, 1)...  42.6 us
    all_to_all x1, waiting for transfers between devices, body(): some_queries = lax.all_to_all(pieces, ('far', 'core'), 0, 0, tiled=True)  25.6 us
    all_to_all x1, blocking collectives, body(): lax.all_to_all(terms, ('head', 'core'), 0, 0, tiled=True).sum(axis=0)  14.7 us
    all_to_all x1, starting transfers between devices, body(): some_queries = lax.all_to_all(pieces, ('far', 'core'), 0, 0, tiled=True)  8.26 us
    ppermute x1, waiting for transfers between devices, body(): lent = lax.ppermute(leaving, 'req', [(0, 1), (1, 0)])  6.32 us
    pallas_call x5, Pallas kernels, call(): pl.pallas_call(kernel, in_specs=[pl.BlockSpec(memory_space=pltpu.SMEM if...  5.85 us
    ppermute x1, starting transfers between devices, body(): lent = lax.ppermute(leaving, 'req', [(0, 1), (1, 0)])  5.38 us
  transfers between devices with their start and end apart: 3, of which 2 were waited for; matrix products, arithmetic and copies ran while one was open for 0% of the time, Pallas kernels for 0%

profile of v2, /device:TPU:33, one launch (start us, length us, event | category | flops | bytes accessed | tf_op | source)
XLA Modules:
  0.0 190.5 jit_solution(14672503140041625648)
XLA Ops:
  0.0 1.1 dynamic-slice_bitcast_fusion
  1.1 0.0 copy-start
  1.1 0.0 copy-start.1
  1.1 0.0 copy-start.2
  1.1 5.4 %collective-permute-start = (bf16[1024,256]{1,0:T(8,128)(2,1)S(1)}, bf16[1024,256]{1,0:T(8,128)(2,1)S(1)}, u32[]{:S(2)}, u32[]{:S(2)}) collective-permute-start(bf16[1024,256]{1,0:T(8,128)(2,1)S(1)} %pad_maximum_fusion.1), channel_id=1, source_target_pairs={{0,8},{8,0},{1,9},{9,1},{2,10},{10,2},{3,11},{11,3},{4,12},{12,4},... | collective-permute-start | bytes 1572872 | tf_op jit(solution)/shard_map/ppermute | solution.py:186
  6.6 0.0 copy-done
  6.6 0.0 copy-done.1
  6.6 0.1 dynamic-slice_bitcast_fusion.2
  6.7 0.0 copy-done.2
  6.8 6.3 %collective-permute-done.lent = bf16[1024,256]{1,0:T(8,128)(2,1)S(1)} collective-permute-done((bf16[1024,256]{1,0:T(8,128)(2,1)S(1)}, bf16[1024,256]{1,0:T(8,128)(2,1)S(1)}, u32[]{:S(2)}, u32[]{:S(2)}) %collective-permute-start) | collective-permute-done | bytes 524320 | tf_op jit(solution)/shard_map/ppermute | solution.py:186
  13.1 0.0 copy-start.4
  13.1 0.9 pad_maximum_fusion
  14.1 42.6 %collective-permute-start.1 = (bf16[3072,128]{1,0:T(8,128)(2,1)}, bf16[3072,128]{1,0:T(8,128)(2,1)S(1)}, u32[]{:S(2)}, u32[]{:S(2)}) collective-permute-start(bf16[3072,128]{1,0:T(8,128)(2,1)} %pad_maximum_fusion), channel_id=1, source_target_pairs={{0,4},{4,0},{1,5},{5,1},{2,6},{6,2},{3,7},{7,3},{8,12},{12,8},{9,1... | collective-permute-start | bytes 2359304 | tf_op jit(solution)/shard_map/ppermute | solution.py:189
  56.7 0.0 copy-done.4
  56.7 0.6 shard_map.55
  57.4 8.3 %all-to-all-start = ((bf16[16,16,128]{2,1,0:T(8,128)(2,1)}), bf16[16,16,128]{2,1,0:T(8,128)(2,1)S(1)}, u32[]{:S(2)}, u32[]{:S(2)}) async-start(bf16[16,16,128]{2,1,0:T(8,128)(2,1)} %shard_map.55), calls=%async_computation | async-start | bytes 131072 | tf_op jit(solution)/shard_map/all_to_all | solution.py:195
  65.6 0.6 stack.27.place
  66.2 25.6 %all-to-all-done = bf16[16,16,128]{2,1,0:T(8,128)(2,1)S(1)} async-done(((bf16[16,16,128]{2,1,0:T(8,128)(2,1)}), bf16[16,16,128]{2,1,0:T(8,128)(2,1)S(1)}, u32[]{:S(2)}, u32[]{:S(2)}) %all-to-all-start) | async-done | bytes 65568 | tf_op jit(solution)/shard_map/all_to_all | solution.py:195
  91.9 0.0 collective-permute-done.1.other
  91.9 8.7 %all_to_all.35 = bf16[4,128,128]{2,1,0:T(8,128)(2,1)S(1)} all-to-all(bf16[4,128,128]{2,1,0:T(8,128)(2,1)S(1)} %bitcast.38), channel_id=1, replica_groups=mesh['groups'=2,'far'=8,'half'=2,'req'=2,'core'=2,'head'=4] {'half','req'}, dimensions={0} | all-to-all | bytes 262144 | tf_op jit(solution)/shard_map/all_to_all | solution.py:158
  100.6 3.9 %shard_map.56 = bf16[2,8,5,8,128]{4,3,2,1,0:T(8,128)(2,1)S(1)} custom-call(s32[6]{0:T(128)} %stack.27.place, s32[2]{0:T(128)} %lengths.1, bf16[64,8,128]{2,1,0:T(8,128)(2,1)S(1)} %bitcast.33, bf16[2,512,256]{2,1,0:T(8,128)(2,1)S(1)} %copy-done, bf16[2,512,256]{2,1,0:T(8,128)(2,1)S(1)} %copy-done.1, bf16[1024,256]{1,0:T(8,128)(2,1)S(1)} %collective-permute-done.lent, ...), custom_call_target="tpu_custom_call" | custom-call | tf_op jit(solution)/shard_map/pallas_call | solution.py:29
  104.5 9.5 %all_to_all.36 = bf16[2,320,128]{2,1,0:T(8,128)(2,1)S(1)} all-to-all(bf16[2,320,128]{2,1,0:T(8,128)(2,1)S(1)} %bitcast.31), channel_id=1, replica_groups=mesh['groups'=2,'far'=8,'half'=2,'req'=2,'core'=2,'head'=4] {'half'}, dimensions={0} | all-to-all | bytes 327680 | tf_op jit(solution)/shard_map/all_to_all | solution.py:158
  114.0 0.0 copy-start.3
  114.0 0.2 shard_map.57
  114.2 24.3 %all_to_all.37 = bf16[8,40,128]{2,1,0:T(8,128)(2,1)S(1)} all-to-all(bf16[8,40,128]{2,1,0:T(8,128)(2,1)S(1)} %bitcast.35), channel_id=1, replica_groups=mesh['groups'=2,'far'=8,'half'=2,'req'=2,'core'=2,'head'=4] {'far'}, dimensions={0} | all-to-all | bytes 163840 | tf_op jit(solution)/shard_map/all_to_all | solution.py:158
  138.5 0.2 shard_map.58
  138.7 26.1 %all_to_all.38 = bf16[8,32,128]{2,1,0:T(8,128)(2,1)S(1)} all-to-all(bf16[8,32,128]{2,1,0:T(8,128)(2,1)S(1)} %bitcast.36), channel_id=1, replica_groups=mesh['groups'=2,'far'=8,'half'=2,'req'=2,'core'=2,'head'=4] {'far'}, dimensions={0} | all-to-all | bytes 131072 | tf_op jit(solution)/shard_map/all_to_all | solution.py:158
  164.8 9.3 %all_to_all.39 = bf16[4,256,128]{2,1,0:T(8,128)(2,1)S(1)} all-to-all(bf16[4,256,128]{2,1,0:T(8,128)(2,1)S(1)} %broadcast_in_dim.15), channel_id=1, replica_groups=mesh['groups'=2,'far'=8,'half'=2,'req'=2,'core'=2,'head'=4] {'half','req'}, dimensions={0} | all-to-all | bytes 524288 | tf_op jit(solution)/shard_map/all_to_all | solution.py:158
  174.2 0.0 copy-done.3
  174.2 1.0 shard_map.59
  175.2 14.7 %all_to_all.40 = f32[8,32,128]{2,1,0:T(8,128)S(1)} all-to-all(f32[8,32,128]{2,1,0:T(8,128)S(1)} %shard_map.59), channel_id=1, replica_groups=mesh['groups'=2,'far'=8,'half'=2,'req'=2,'core'=2,'head'=4] {'head','core'}, dimensions={0} | all-to-all | bytes 262144 | tf_op jit(solution)/shard_map/all_to_all | solution.py:216
  189.9 0.6 copy.8
  (7 shorter events, 0.2 us)
Async XLA Ops:
  1.1 5.5 %copy-start = (bf16[2,512,256]{2,1,0:T(8,128)(2,1)S(1)}, bf16[2,512,256]{2,1,0:T(8,128)(2,1)}, u32[]{:S(2)}) copy-start(bf16[2,512,256]{2,1,0:T(8,128)(2,1)} %own_keys.1) | copy-start | bytes 1572868
  1.1 5.5 %copy-start.1 = (bf16[2,512,256]{2,1,0:T(8,128)(2,1)S(1)}, bf16[2,512,256]{2,1,0:T(8,128)(2,1)}, u32[]{:S(2)}) copy-start(bf16[2,512,256]{2,1,0:T(8,128)(2,1)} %own_values.1) | copy-start | bytes 1572868
  1.1 5.6 %copy-start.2 = (bf16[2048,128]{1,0:T(8,128)(2,1)S(1)}, bf16[2048,128]{1,0:T(8,128)(2,1)}, u32[]{:S(2)}) copy-start(bf16[2048,128]{1,0:T(8,128)(2,1)} %weight.1) | copy-start | bytes 1572868
  1.1 11.9 %collective-permute-start = (bf16[1024,256]{1,0:T(8,128)(2,1)S(1)}, bf16[1024,256]{1,0:T(8,128)(2,1)S(1)}, u32[]{:S(2)}, u32[]{:S(2)}) collective-permute-start(bf16[1024,256]{1,0:T(8,128)(2,1)S(1)} %pad_maximum_fusion.1), channel_id=1, source_target_pairs={{0,8},{8,0},{1,9},{9,1},{2,10},{10,2},{3,11},{11,3},{4,12},{12,4},... | collective-permute-start | bytes 1572872 | tf_op jit(solution)/shard_map/ppermute | solution.py:186
  13.1 43.6 %copy-start.4 = (bf16[2,1,2048]{2,0,1:T(2,128)(2,1)S(1)}, bf16[2,1,2048]{2,0,1:T(2,128)(2,1)}, u32[]{:S(2)}) copy-start(bf16[2,1,2048]{2,0,1:T(2,128)(2,1)} %param.5) | copy-start | bytes 24580
  14.1 77.8 %collective-permute-start.1 = (bf16[3072,128]{1,0:T(8,128)(2,1)}, bf16[3072,128]{1,0:T(8,128)(2,1)S(1)}, u32[]{:S(2)}, u32[]{:S(2)}) collective-permute-start(bf16[3072,128]{1,0:T(8,128)(2,1)} %pad_maximum_fusion), channel_id=1, source_target_pairs={{0,4},{4,0},{1,5},{5,1},{2,6},{6,2},{3,7},{7,3},{8,12},{12,8},{9,1... | collective-permute-start | bytes 2359304 | tf_op jit(solution)/shard_map/ppermute | solution.py:189
  57.4 34.5 %all-to-all-start = ((bf16[16,16,128]{2,1,0:T(8,128)(2,1)}), bf16[16,16,128]{2,1,0:T(8,128)(2,1)S(1)}, u32[]{:S(2)}, u32[]{:S(2)}) async-start(bf16[16,16,128]{2,1,0:T(8,128)(2,1)} %shard_map.55), calls=%async_computation | async-start | bytes 131072 | tf_op jit(solution)/shard_map/all_to_all | solution.py:195
  114.0 60.2 %copy-start.3 = (bf16[2048,128]{1,0:T(8,128)(2,1)S(1)}, bf16[2048,128]{1,0:T(8,128)(2,1)}, u32[]{:S(2)}) copy-start(bf16[2048,128]{1,0:T(8,128)(2,1)} %weight.1) | copy-start | bytes 1572868

commit v3 on v2

--- a/solution.py
+++ b/solution.py
@@ -61,9 +61,10 @@
     scale = 1.0 / math.sqrt(dim)
     core, request = place[0], place[1]
     head = pl.ds(pl.multiple_of(core * dim, dim), dim)
-    row = lax.broadcasted_iota(jnp.int32, (rows, span), 0) // group
+    row = lax.broadcasted_iota(jnp.int32, (rows, dim), 0) // group
     token = row // CORES % far * (NEAR * CORES) + row // (far * CORES) * CORES + row % CORES
-    ahead = lax.broadcasted_iota(jnp.int32, (rows, span), 1) - token
+    before = lax.broadcasted_iota(jnp.int32, (rows, dim), 1) - token
+    ahead = jnp.concatenate([before + at for at in range(0, span, dim)], axis=1)
     q = queries[...].astype(f32).reshape(rows, dim).astype(bf16)
     last = lengths[request] - new_count
     keys = [own_keys[request, :, head], other[:span, :], lent[:span, head], other[2 * span : 3 * span, :]]

time: 191 us -> 191 us (level)
  no operation moved by 1% of the time
where the time goes in v3:
time: 191 us
  blocking collectives  92.7 us (49%)
  starting transfers between devices  56.3 us (29%)
  waiting for transfers between devices  32 us (17%)
  Pallas kernels  5.87 us (3%)
  local copies, waits for them, and re-layouts  2.55 us (1%)
    all_to_all x5, blocking collectives, exchanged(): return lax.all_to_all(flat, axes, 0, 0, tiled=True).reshape(pieces.shape)  78 us
    ppermute x1, starting transfers between devices, body(): lax.ppermute(jnp.concatenate([*leaving, theirs], axis=0), 'core', [(0, 1)...  42.6 us
    all_to_all x1, waiting for transfers between devices, body(): some_queries = lax.all_to_all(pieces, ('far', 'core'), 0, 0, tiled=True)  25.6 us
    all_to_all x1, blocking collectives, body(): lax.all_to_all(terms, ('head', 'core'), 0, 0, tiled=True).sum(axis=0)  14.7 us
    all_to_all x1, starting transfers between devices, body(): some_queries = lax.all_to_all(pieces, ('far', 'core'), 0, 0, tiled=True)  8.26 us
    ppermute x1, waiting for transfers between devices, body(): lent = lax.ppermute(leaving, 'req', [(0, 1), (1, 0)])  6.32 us
    pallas_call x5, Pallas kernels, call(): pl.pallas_call(kernel, in_specs=[pl.BlockSpec(memory_space=pltpu.SMEM if...  5.87 us
    ppermute x1, starting transfers between devices, body(): lent = lax.ppermute(leaving, 'req', [(0, 1), (1, 0)])  5.38 us
  transfers between devices with their start and end apart: 3, of which 2 were waited for; matrix products, arithmetic and copies ran while one was open for 0% of the time, Pallas kernels for 0%

profile of v3, /device:TPU:33, one launch (start us, length us, event | category | flops | bytes accessed | tf_op | source)
XLA Modules:
  0.0 190.5 jit_solution(14282147126621763182)
XLA Ops:
  0.0 1.1 dynamic-slice_bitcast_fusion
  1.1 0.0 copy-start
  1.1 0.0 copy-start.1
  1.1 0.0 copy-start.2
  1.1 5.4 %collective-permute-start = (bf16[1024,256]{1,0:T(8,128)(2,1)S(1)}, bf16[1024,256]{1,0:T(8,128)(2,1)S(1)}, u32[]{:S(2)}, u32[]{:S(2)}) collective-permute-start(bf16[1024,256]{1,0:T(8,128)(2,1)S(1)} %pad_maximum_fusion.1), channel_id=1, source_target_pairs={{0,8},{8,0},{1,9},{9,1},{2,10},{10,2},{3,11},{11,3},{4,12},{12,4},... | collective-permute-start | bytes 1572872 | tf_op jit(solution)/shard_map/ppermute | solution.py:187
  6.6 0.0 copy-done
  6.6 0.0 copy-done.1
  6.6 0.1 dynamic-slice_bitcast_fusion.2
  6.7 0.0 copy-done.2
  6.8 6.3 %collective-permute-done.lent = bf16[1024,256]{1,0:T(8,128)(2,1)S(1)} collective-permute-done((bf16[1024,256]{1,0:T(8,128)(2,1)S(1)}, bf16[1024,256]{1,0:T(8,128)(2,1)S(1)}, u32[]{:S(2)}, u32[]{:S(2)}) %collective-permute-start) | collective-permute-done | bytes 524320 | tf_op jit(solution)/shard_map/ppermute | solution.py:187
  13.1 0.0 copy-start.4
  13.1 0.9 pad_maximum_fusion
  14.1 42.6 %collective-permute-start.1 = (bf16[3072,128]{1,0:T(8,128)(2,1)}, bf16[3072,128]{1,0:T(8,128)(2,1)S(1)}, u32[]{:S(2)}, u32[]{:S(2)}) collective-permute-start(bf16[3072,128]{1,0:T(8,128)(2,1)} %pad_maximum_fusion), channel_id=1, source_target_pairs={{0,4},{4,0},{1,5},{5,1},{2,6},{6,2},{3,7},{7,3},{8,12},{12,8},{9,1... | collective-permute-start | bytes 2359304 | tf_op jit(solution)/shard_map/ppermute | solution.py:190
  56.7 0.0 copy-done.4
  56.7 0.6 shard_map.55
  57.4 8.3 %all-to-all-start = ((bf16[16,16,128]{2,1,0:T(8,128)(2,1)}), bf16[16,16,128]{2,1,0:T(8,128)(2,1)S(1)}, u32[]{:S(2)}, u32[]{:S(2)}) async-start(bf16[16,16,128]{2,1,0:T(8,128)(2,1)} %shard_map.55), calls=%async_computation | async-start | bytes 131072 | tf_op jit(solution)/shard_map/all_to_all | solution.py:196
  65.6 0.6 stack.27.place
  66.2 25.6 %all-to-all-done = bf16[16,16,128]{2,1,0:T(8,128)(2,1)S(1)} async-done(((bf16[16,16,128]{2,1,0:T(8,128)(2,1)}), bf16[16,16,128]{2,1,0:T(8,128)(2,1)S(1)}, u32[]{:S(2)}, u32[]{:S(2)}) %all-to-all-start) | async-done | bytes 65568 | tf_op jit(solution)/shard_map/all_to_all | solution.py:196
  91.9 0.0 collective-permute-done.1.other
  91.9 8.7 %all_to_all.35 = bf16[4,128,128]{2,1,0:T(8,128)(2,1)S(1)} all-to-all(bf16[4,128,128]{2,1,0:T(8,128)(2,1)S(1)} %bitcast.38), channel_id=1, replica_groups=mesh['groups'=2,'far'=8,'half'=2,'req'=2,'core'=2,'head'=4] {'half','req'}, dimensions={0} | all-to-all | bytes 262144 | tf_op jit(solution)/shard_map/all_to_all | solution.py:159
  100.6 3.9 %shard_map.56 = bf16[2,8,5,8,128]{4,3,2,1,0:T(8,128)(2,1)S(1)} custom-call(s32[6]{0:T(128)} %stack.27.place, s32[2]{0:T(128)} %lengths.1, bf16[64,8,128]{2,1,0:T(8,128)(2,1)S(1)} %bitcast.33, bf16[2,512,256]{2,1,0:T(8,128)(2,1)S(1)} %copy-done, bf16[2,512,256]{2,1,0:T(8,128)(2,1)S(1)} %copy-done.1, bf16[1024,256]{1,0:T(8,128)(2,1)S(1)} %collective-permute-done.lent, ...), custom_call_target="tpu_custom_call" | custom-call | tf_op jit(solution)/shard_map/pallas_call | solution.py:29
  104.5 9.5 %all_to_all.36 = bf16[2,320,128]{2,1,0:T(8,128)(2,1)S(1)} all-to-all(bf16[2,320,128]{2,1,0:T(8,128)(2,1)S(1)} %bitcast.31), channel_id=1, replica_groups=mesh['groups'=2,'far'=8,'half'=2,'req'=2,'core'=2,'head'=4] {'half'}, dimensions={0} | all-to-all | bytes 327680 | tf_op jit(solution)/shard_map/all_to_all | solution.py:159
  114.0 0.0 copy-start.3
  114.0 0.2 shard_map.57
  114.2 24.3 %all_to_all.37 = bf16[8,40,128]{2,1,0:T(8,128)(2,1)S(1)} all-to-all(bf16[8,40,128]{2,1,0:T(8,128)(2,1)S(1)} %bitcast.35), channel_id=1, replica_groups=mesh['groups'=2,'far'=8,'half'=2,'req'=2,'core'=2,'head'=4] {'far'}, dimensions={0} | all-to-all | bytes 163840 | tf_op jit(solution)/shard_map/all_to_all | solution.py:159
  138.5 0.2 shard_map.58
  138.7 26.1 %all_to_all.38 = bf16[8,32,128]{2,1,0:T(8,128)(2,1)S(1)} all-to-all(bf16[8,32,128]{2,1,0:T(8,128)(2,1)S(1)} %bitcast.36), channel_id=1, replica_groups=mesh['groups'=2,'far'=8,'half'=2,'req'=2,'core'=2,'head'=4] {'far'}, dimensions={0} | all-to-all | bytes 131072 | tf_op jit(solution)/shard_map/all_to_all | solution.py:159
  164.9 9.3 %all_to_all.39 = bf16[4,256,128]{2,1,0:T(8,128)(2,1)S(1)} all-to-all(bf16[4,256,128]{2,1,0:T(8,128)(2,1)S(1)} %broadcast_in_dim.15), channel_id=1, replica_groups=mesh['groups'=2,'far'=8,'half'=2,'req'=2,'core'=2,'head'=4] {'half','req'}, dimensions={0} | all-to-all | bytes 524288 | tf_op jit(solution)/shard_map/all_to_all | solution.py:159
  174.2 0.0 copy-done.3
  174.2 1.0 shard_map.59
  175.2 14.7 %all_to_all.40 = f32[8,32,128]{2,1,0:T(8,128)S(1)} all-to-all(f32[8,32,128]{2,1,0:T(8,128)S(1)} %shard_map.59), channel_id=1, replica_groups=mesh['groups'=2,'far'=8,'half'=2,'req'=2,'core'=2,'head'=4] {'head','core'}, dimensions={0} | all-to-all | bytes 262144 | tf_op jit(solution)/shard_map/all_to_all | solution.py:217
  189.9 0.6 copy.8
  (7 shorter events, 0.2 us)
Async XLA Ops:
  1.1 5.5 %copy-start = (bf16[2,512,256]{2,1,0:T(8,128)(2,1)S(1)}, bf16[2,512,256]{2,1,0:T(8,128)(2,1)}, u32[]{:S(2)}) copy-start(bf16[2,512,256]{2,1,0:T(8,128)(2,1)} %own_keys.1) | copy-start | bytes 1572868
  1.1 5.5 %copy-start.1 = (bf16[2,512,256]{2,1,0:T(8,128)(2,1)S(1)}, bf16[2,512,256]{2,1,0:T(8,128)(2,1)}, u32[]{:S(2)}) copy-start(bf16[2,512,256]{2,1,0:T(8,128)(2,1)} %own_values.1) | copy-start | bytes 1572868
  1.1 5.6 %copy-start.2 = (bf16[2048,128]{1,0:T(8,128)(2,1)S(1)}, bf16[2048,128]{1,0:T(8,128)(2,1)}, u32[]{:S(2)}) copy-start(bf16[2048,128]{1,0:T(8,128)(2,1)} %weight.1) | copy-start | bytes 1572868
  1.1 11.9 %collective-permute-start = (bf16[1024,256]{1,0:T(8,128)(2,1)S(1)}, bf16[1024,256]{1,0:T(8,128)(2,1)S(1)}, u32[]{:S(2)}, u32[]{:S(2)}) collective-permute-start(bf16[1024,256]{1,0:T(8,128)(2,1)S(1)} %pad_maximum_fusion.1), channel_id=1, source_target_pairs={{0,8},{8,0},{1,9},{9,1},{2,10},{10,2},{3,11},{11,3},{4,12},{12,4},... | collective-permute-start | bytes 1572872 | tf_op jit(solution)/shard_map/ppermute | solution.py:187
  13.1 43.6 %copy-start.4 = (bf16[2,1,2048]{2,0,1:T(2,128)(2,1)S(1)}, bf16[2,1,2048]{2,0,1:T(2,128)(2,1)}, u32[]{:S(2)}) copy-start(bf16[2,1,2048]{2,0,1:T(2,128)(2,1)} %param.5) | copy-start | bytes 24580
  14.1 77.8 %collective-permute-start.1 = (bf16[3072,128]{1,0:T(8,128)(2,1)}, bf16[3072,128]{1,0:T(8,128)(2,1)S(1)}, u32[]{:S(2)}, u32[]{:S(2)}) collective-permute-start(bf16[3072,128]{1,0:T(8,128)(2,1)} %pad_maximum_fusion), channel_id=1, source_target_pairs={{0,4},{4,0},{1,5},{5,1},{2,6},{6,2},{3,7},{7,3},{8,12},{12,8},{9,1... | collective-permute-start | bytes 2359304 | tf_op jit(solution)/shard_map/ppermute | solution.py:190
  57.4 34.5 %all-to-all-start = ((bf16[16,16,128]{2,1,0:T(8,128)(2,1)}), bf16[16,16,128]{2,1,0:T(8,128)(2,1)S(1)}, u32[]{:S(2)}, u32[]{:S(2)}) async-start(bf16[16,16,128]{2,1,0:T(8,128)(2,1)} %shard_map.55), calls=%async_computation | async-start | bytes 131072 | tf_op jit(solution)/shard_map/all_to_all | solution.py:196
  114.0 60.2 %copy-start.3 = (bf16[2048,128]{1,0:T(8,128)(2,1)S(1)}, bf16[2048,128]{1,0:T(8,128)(2,1)}, u32[]{:S(2)}) copy-start(bf16[2048,128]{1,0:T(8,128)(2,1)} %weight.1) | copy-start | bytes 1572868

commit v4 on v3

--- a/solution.py
+++ b/solution.py
@@ -52,14 +52,16 @@
             out[p] = piece
 
 
-def attention_kernel(place, lengths, queries, own_keys, own_values, lent, other, out):
+def attention_kernel(lengths, queries, own_keys, own_values, lent, other, out):
     new_count, group, dim = queries.shape
     halves, far, kept = out.shape[0], out.shape[1], out.shape[2] - 1
     span = own_keys.shape[1]
     rows = new_count * group
     inner = NEAR // halves
     scale = 1.0 / math.sqrt(dim)
-    core, request = place[0], place[1]
+    core, request = lax.axis_index("core"), lax.axis_index("req")
+    z = lax.axis_index("far") * NEAR + lax.axis_index("half") * REQUESTS + request
+    blocks = [(a * CORES + c) * span for a in (z, z + 1 - 2 * request) for c in (core, 1 - core)]
     head = pl.ds(pl.multiple_of(core * dim, dim), dim)
     row = lax.broadcasted_iota(jnp.int32, (rows, dim), 0) // group
     token = row // CORES % far * (NEAR * CORES) + row // (far * CORES) * CORES + row % CORES
@@ -73,7 +75,7 @@
     scores = []
     for part, k in enumerate(keys):
         s = lax.dot_general(q, k, (((1,), (1,)), ((), ())), preferred_element_type=f32)
-        scores.append(jnp.where(ahead <= last - place[2 + part], s * scale, masked_fill_value))
+        scores.append(jnp.where(ahead <= last - blocks[part], s * scale, masked_fill_value))
     shift = jnp.max(functools.reduce(jnp.maximum, scores), axis=1, keepdims=True)
     shift = shift.astype(bf16).astype(f32)
     lowest = jnp.maximum(shift, 0.1 * masked_fill_value)
@@ -130,7 +132,7 @@
         out[:, k] = jnp.broadcast_to(row[None], (out.shape[0], *row.shape))
 
 
-def project_kernel(place, attention, weight, other, out, wide):
+def project_kernel(attention, weight, other, out, wide):
     pieces, per_piece, _ = out.shape
     inputs, dim = weight.shape[0] // CORES, attention.shape[1]
     group = inputs // dim
@@ -146,9 +148,10 @@
     left = jnp.concatenate(
         [wide[pl.ds(h, rows, stride=group), :].astype(bf16) for h in range(group)], axis=1
     )
-    mine = weight[pl.ds(pl.multiple_of(place[0] * inputs, inputs), inputs), :]
+    own_core = lax.axis_index("core")
+    mine = weight[pl.ds(pl.multiple_of(own_core * inputs, inputs), inputs), :]
     theirs = other[other.shape[0] - inputs :, :]
-    for right, core in ((mine, place[0]), (theirs, 1 - place[0])):
+    for right, core in ((mine, own_core), (theirs, 1 - own_core)):
         terms = jnp.dot(left, right, preferred_element_type=f32)
         for x in range(pieces // CORES):
             out[x * CORES + core] = terms[x * per_piece : (x + 1) * per_piece]
@@ -164,7 +167,7 @@
 
 
 def body(queries, stored_cache_keys, stored_cache_values, out_weight, lengths):
-    requests, span, _ = stored_cache_keys.shape
+    requests, _, _ = stored_cache_keys.shape
     far_count, x_count = lax.axis_size("far"), lax.axis_size("head")
     z_count = far_count * NEAR
     new_count = queries.shape[1] * z_count * CORES
@@ -172,7 +175,7 @@
     group = queries.shape[2] // (CORES * dim)
     inputs = out_weight.shape[0] // CORES
     columns = out_weight.shape[1]
-    z, core, req = lax.axis_index(("far", *NEAR_AXES)), lax.axis_index("core"), lax.axis_index("req")
+    core, req = lax.axis_index("core"), lax.axis_index("req")
     kept = NEAR // HALVES * CORES
     rows = new_count * requests
 
@@ -189,18 +192,15 @@
     leaving = [head_of(a, 1 - core) for a in (*(of_request(a, req) for a in caches), lent)]
     other = lax.ppermute(jnp.concatenate([*leaving, theirs], axis=0), "core", [(0, 1), (1, 0)])
 
-    other_z = z + 1 - 2 * req
-    first = [z * CORES + core, z * CORES + 1 - core, other_z * CORES + core, other_z * CORES + 1 - core]
-    place = jnp.stack([core, req, *(b * span for b in first)]).astype(jnp.int32)
     pieces = in_vmem(spread_kernel, (far_count * CORES, requests * group, dim), bf16)(queries.reshape(requests, -1))
     some_queries = lax.all_to_all(pieces, ("far", "core"), 0, 0, tiled=True)
-    some_queries, lent, other, place = lax.optimization_barrier((some_queries, lent, other, place))
+    some_queries, lent, other = lax.optimization_barrier((some_queries, lent, other))
     pieces = some_queries.reshape(-1, requests, group, dim).transpose(1, 0, 2, 3)
     pieces = jnp.broadcast_to(pieces[None], (HALVES, *pieces.shape)).reshape(NEAR, *pieces.shape[1:])
     all_queries = exchanged(pieces, NEAR_AXES).reshape(new_count, group, dim)
 
     partial = in_vmem(attention_kernel, (HALVES, far_count, kept + 1, group, dim), bf16)(
-        place, lengths, all_queries, stored_cache_keys, stored_cache_values, lent, other
+        lengths, all_queries, stored_cache_keys, stored_cache_values, lent, other
     )
     partial = in_vmem(merge_near_kernel, partial.shape[1:], bf16)(exchanged(partial, "half"))
     own = in_vmem(merge_far_kernel, (far_count, kept, group, dim), bf16)(
@@ -213,7 +213,7 @@
         (x_count * CORES, rows // x_count, columns),
         f32,
         scratch_shapes=[pltpu.VMEM((rows * group, dim), f32)],
-    )(place, attention.reshape(rows * group, dim), out_weight, other)
+    )(attention.reshape(rows * group, dim), out_weight, other)
     terms = lax.all_to_all(terms, ("head", "core"), 0, 0, tiled=True).sum(axis=0)
     terms = terms.reshape(-1, requests, columns).transpose(1, 0, 2)
     return terms.astype(bf16)

time: 191 us -> 190 us (level)
  blocking collectives: 92.7 us -> 127 us
  waiting for transfers between devices: 32 us -> 6.32 us
  starting transfers between devices: 56.3 us -> 48 us
    all_to_all x0 -> x1, blocking collectives: none -> 34.3 us  [body(): some_queries = lax.all_to_all(pieces, ('far', 'core'), 0, 0, tiled=True)]
    all_to_all x1 -> x0, waiting for transfers between devices: 25.6 us -> none  [body(): some_queries = lax.all_to_all(pieces, ('far', 'core'), 0, 0, tiled=True)]
    all_to_all x1 -> x0, starting transfers between devices: 8.26 us -> none  [body(): some_queries = lax.all_to_all(pieces, ('far', 'core'), 0, 0, tiled=True)]
  transfers between devices with their start and end apart: 3 -> 2, of which waited for: 2 -> 1; matrix products, arithmetic and copies ran while one was open for 0% -> 0% of each run, Pallas kernels for 0% -> 0%
where the time goes in v4:
time: 190 us; the launch traced here: 189 us
  blocking collectives  127 us (67%)
  starting transfers between devices  48 us (25%)
  waiting for transfers between devices  6.32 us (3%)
  Pallas kernels  4.57 us (2%)
  local copies, waits for them, and re-layouts  1.95 us (1%)
    all_to_all x5, blocking collectives, exchanged(): return lax.all_to_all(flat, axes, 0, 0, tiled=True).reshape(pieces.shape)  78 us
    ppermute x1, starting transfers between devices, body(): lax.ppermute(jnp.concatenate([*leaving, theirs], axis=0), 'core', [(0, 1)...  42.6 us
    all_to_all x1, blocking collectives, body(): some_queries = lax.all_to_all(pieces, ('far', 'core'), 0, 0, tiled=True)  34.3 us
    all_to_all x1, blocking collectives, body(): lax.all_to_all(terms, ('head', 'core'), 0, 0, tiled=True).sum(axis=0)  14.8 us
    ppermute x1, waiting for transfers between devices, body(): lent = lax.ppermute(leaving, 'req', [(0, 1), (1, 0)])  6.32 us
    ppermute x1, starting transfers between devices, body(): lent = lax.ppermute(leaving, 'req', [(0, 1), (1, 0)])  5.38 us
    pallas_call x5, Pallas kernels, call(): pl.pallas_call(kernel, in_specs=[pl.BlockSpec(memory_space=pltpu.SMEM if...  4.57 us
  transfers between devices with their start and end apart: 2, of which 1 were waited for; matrix products, arithmetic and copies ran while one was open for 0% of the time, Pallas kernels for 0%

profile of v4, /device:TPU:33, one launch (start us, length us, event | category | flops | bytes accessed | tf_op | source)
XLA Modules:
  0.0 189.1 jit_solution(12942543059994857271)
XLA Ops:
  0.0 1.1 dynamic-slice_bitcast_fusion
  1.1 0.0 copy-start
  1.1 0.0 copy-start.1
  1.1 0.0 copy-start.2
  1.1 5.4 %collective-permute-start = (bf16[1024,256]{1,0:T(8,128)(2,1)S(1)}, bf16[1024,256]{1,0:T(8,128)(2,1)S(1)}, u32[]{:S(2)}, u32[]{:S(2)}) collective-permute-start(bf16[1024,256]{1,0:T(8,128)(2,1)S(1)} %pad_maximum_fusion.1), channel_id=1, source_target_pairs={{0,8},{8,0},{1,9},{9,1},{2,10},{10,2},{3,11},{11,3},{4,12},{12,4},... | collective-permute-start | bytes 1572872 | tf_op jit(solution)/shard_map/ppermute | solution.py:190
  6.6 0.0 copy-done
  6.6 0.0 copy-done.1
  6.6 0.1 dynamic-slice_bitcast_fusion.2
  6.7 0.0 copy-done.2
  6.8 6.3 %collective-permute-done.lent = bf16[1024,256]{1,0:T(8,128)(2,1)S(1)} collective-permute-done((bf16[1024,256]{1,0:T(8,128)(2,1)S(1)}, bf16[1024,256]{1,0:T(8,128)(2,1)S(1)}, u32[]{:S(2)}, u32[]{:S(2)}) %collective-permute-start) | collective-permute-done | bytes 524320 | tf_op jit(solution)/shard_map/ppermute | solution.py:190
  13.1 0.0 copy-start.4
  13.1 0.9 pad_maximum_fusion
  14.1 42.6 %collective-permute-start.1 = (bf16[3072,128]{1,0:T(8,128)(2,1)}, bf16[3072,128]{1,0:T(8,128)(2,1)S(1)}, u32[]{:S(2)}, u32[]{:S(2)}) collective-permute-start(bf16[3072,128]{1,0:T(8,128)(2,1)} %pad_maximum_fusion), channel_id=1, source_target_pairs={{0,4},{4,0},{1,5},{5,1},{2,6},{6,2},{3,7},{7,3},{8,12},{12,8},{9,1... | collective-permute-start | bytes 2359304 | tf_op jit(solution)/shard_map/ppermute | solution.py:193
  56.7 0.0 copy-done.4
  56.8 34.3 %all_to_all.35 = bf16[16,16,128]{2,1,0:T(8,128)(2,1)S(1)} all-to-all(bf16[16,16,128]{2,1,0:T(8,128)(2,1)S(1)} %shard_map.55), channel_id=1, replica_groups=mesh['groups'=2,'far'=8,'half'=2,'req'=2,'core'=2,'head'=4] {'far','core'}, dimensions={0} | all-to-all | bytes 131072 | tf_op jit(solution)/shard_map/all_to_all | solution.py:196
  91.0 0.0 collective-permute-done.1.other
  91.1 8.7 %all_to_all.36 = bf16[4,128,128]{2,1,0:T(8,128)(2,1)S(1)} all-to-all(bf16[4,128,128]{2,1,0:T(8,128)(2,1)S(1)} %bitcast.32), channel_id=1, replica_groups=mesh['groups'=2,'far'=8,'half'=2,'req'=2,'core'=2,'head'=4] {'half','req'}, dimensions={0} | all-to-all | bytes 262144 | tf_op jit(solution)/shard_map/all_to_all | solution.py:162
  99.8 3.9 %shard_map.56 = bf16[2,8,5,8,128]{4,3,2,1,0:T(8,128)(2,1)S(1)} custom-call(s32[2]{0:T(128)} %lengths.1, bf16[64,8,128]{2,1,0:T(8,128)(2,1)S(1)} %bitcast.27, bf16[2,512,256]{2,1,0:T(8,128)(2,1)S(1)} %copy-done, bf16[2,512,256]{2,1,0:T(8,128)(2,1)S(1)} %copy-done.1, bf16[1024,256]{1,0:T(8,128)(2,1)S(1)} %collective-permute-done.lent, ...), custom_call_target="tpu_custom_call" | custom-call | tf_op jit(solution)/shard_map/pallas_call | solution.py:29
  103.6 9.5 %all_to_all.37 = bf16[2,320,128]{2,1,0:T(8,128)(2,1)S(1)} all-to-all(bf16[2,320,128]{2,1,0:T(8,128)(2,1)S(1)} %bitcast.25), channel_id=1, replica_groups=mesh['groups'=2,'far'=8,'half'=2,'req'=2,'core'=2,'head'=4] {'half'}, dimensions={0} | all-to-all | bytes 327680 | tf_op jit(solution)/shard_map/all_to_all | solution.py:162
  113.2 0.0 copy-start.3
  113.2 0.2 shard_map.57
  113.3 24.3 %all_to_all.38 = bf16[8,40,128]{2,1,0:T(8,128)(2,1)S(1)} all-to-all(bf16[8,40,128]{2,1,0:T(8,128)(2,1)S(1)} %bitcast.29), channel_id=1, replica_groups=mesh['groups'=2,'far'=8,'half'=2,'req'=2,'core'=2,'head'=4] {'far'}, dimensions={0} | all-to-all | bytes 163840 | tf_op jit(solution)/shard_map/all_to_all | solution.py:162
  137.7 0.2 shard_map.58
  137.8 26.2 %all_to_all.39 = bf16[8,32,128]{2,1,0:T(8,128)(2,1)S(1)} all-to-all(bf16[8,32,128]{2,1,0:T(8,128)(2,1)S(1)} %bitcast.30), channel_id=1, replica_groups=mesh['groups'=2,'far'=8,'half'=2,'req'=2,'core'=2,'head'=4] {'far'}, dimensions={0} | all-to-all | bytes 131072 | tf_op jit(solution)/shard_map/all_to_all | solution.py:162
  164.0 9.3 %all_to_all.40 = bf16[4,256,128]{2,1,0:T(8,128)(2,1)S(1)} all-to-all(bf16[4,256,128]{2,1,0:T(8,128)(2,1)S(1)} %broadcast_in_dim.15), channel_id=1, replica_groups=mesh['groups'=2,'far'=8,'half'=2,'req'=2,'core'=2,'head'=4] {'half','req'}, dimensions={0} | all-to-all | bytes 524288 | tf_op jit(solution)/shard_map/all_to_all | solution.py:162
  173.3 0.0 copy-done.3
  173.3 0.3 shard_map.59
  173.7 14.8 %all_to_all.41 = f32[8,32,128]{2,1,0:T(8,128)S(1)} all-to-all(f32[8,32,128]{2,1,0:T(8,128)S(1)} %shard_map.59), channel_id=1, replica_groups=mesh['groups'=2,'far'=8,'half'=2,'req'=2,'core'=2,'head'=4] {'head','core'}, dimensions={0} | all-to-all | bytes 262144 | tf_op jit(solution)/shard_map/all_to_all | solution.py:217
  188.5 0.6 copy.8
  (8 shorter events, 0.2 us)
Async XLA Ops:
  1.1 5.5 %copy-start = (bf16[2,512,256]{2,1,0:T(8,128)(2,1)S(1)}, bf16[2,512,256]{2,1,0:T(8,128)(2,1)}, u32[]{:S(2)}) copy-start(bf16[2,512,256]{2,1,0:T(8,128)(2,1)} %own_keys.1) | copy-start | bytes 1572868
  1.1 5.5 %copy-start.1 = (bf16[2,512,256]{2,1,0:T(8,128)(2,1)S(1)}, bf16[2,512,256]{2,1,0:T(8,128)(2,1)}, u32[]{:S(2)}) copy-start(bf16[2,512,256]{2,1,0:T(8,128)(2,1)} %own_values.1) | copy-start | bytes 1572868
  1.1 5.6 %copy-start.2 = (bf16[2048,128]{1,0:T(8,128)(2,1)S(1)}, bf16[2048,128]{1,0:T(8,128)(2,1)}, u32[]{:S(2)}) copy-start(bf16[2048,128]{1,0:T(8,128)(2,1)} %weight.1) | copy-start | bytes 1572868
  1.1 11.9 %collective-permute-start = (bf16[1024,256]{1,0:T(8,128)(2,1)S(1)}, bf16[1024,256]{1,0:T(8,128)(2,1)S(1)}, u32[]{:S(2)}, u32[]{:S(2)}) collective-permute-start(bf16[1024,256]{1,0:T(8,128)(2,1)S(1)} %pad_maximum_fusion.1), channel_id=1, source_target_pairs={{0,8},{8,0},{1,9},{9,1},{2,10},{10,2},{3,11},{11,3},{4,12},{12,4},... | collective-permute-start | bytes 1572872 | tf_op jit(solution)/shard_map/ppermute | solution.py:190
  13.1 43.6 %copy-start.4 = (bf16[2,1,2048]{2,0,1:T(2,128)(2,1)S(1)}, bf16[2,1,2048]{2,0,1:T(2,128)(2,1)}, u32[]{:S(2)}) copy-start(bf16[2,1,2048]{2,0,1:T(2,128)(2,1)} %param.5) | copy-start | bytes 24580
  14.1 77.0 %collective-permute-start.1 = (bf16[3072,128]{1,0:T(8,128)(2,1)}, bf16[3072,128]{1,0:T(8,128)(2,1)S(1)}, u32[]{:S(2)}, u32[]{:S(2)}) collective-permute-start(bf16[3072,128]{1,0:T(8,128)(2,1)} %pad_maximum_fusion), channel_id=1, source_target_pairs={{0,4},{4,0},{1,5},{5,1},{2,6},{6,2},{3,7},{7,3},{8,12},{12,8},{9,1... | collective-permute-start | bytes 2359304 | tf_op jit(solution)/shard_map/ppermute | solution.py:193
  113.2 60.2 %copy-start.3 = (bf16[2048,128]{1,0:T(8,128)(2,1)S(1)}, bf16[2048,128]{1,0:T(8,128)(2,1)}, u32[]{:S(2)}) copy-start(bf16[2048,128]{1,0:T(8,128)(2,1)} %weight.1) | copy-start | bytes 1572868
